TPU v7x, 32 devices: a whole 2x2x4 slice. The times are simulated.
32 devices in a mesh: vocab: 8 (over y, x, core), hid: 4 (over z).
Axes of the slice: x: 2, y: 2, z: 4, core: 2. Of those that a mesh axis runs over, the one named last changes fastest.
Arguments:
- hidden: bfloat16 [2, 256, 7168], P(None, 'vocab', 'hid'), may hold values from -100 to 100
- head_weight: bfloat16 [7168, 65536], P('hid', 'vocab'), may hold values from -2 to 2
- targets: int32 [2, 256], P(None, 'hid'), may hold values from 0 to 65535
Outputs:
- entropy: float32 [2, 256], P(None, 'hid')
- squared: float32 [2, 256], P(None, 'hid')
All inputs are finite; a program needn't handle non-finite values.
Results may differ from a plain program's by a relative error of at most 0.0003.
Values may be sent and summed in bfloat16 or wider, within the bound.
A program may use at most 192 MiB of HBM per device.

v0:
```python
import jax
import jax.numpy as jnp
from jax import lax
from jax.sharding import PartitionSpec as P


def peak_and_picked(logits, labels, first_column):
    column_ids = first_column + lax.broadcasted_iota(jnp.int32, logits.shape, logits.ndim - 1)
    local_peak = jnp.max(logits, axis=-1)
    picked = jnp.sum(jnp.where(column_ids == labels[..., None], logits, 0.0), axis=-1)
    return (local_peak, picked)


def rescaled_sum(logits, peak_value):
    return jnp.sum(jnp.exp(logits - peak_value[..., None]), axis=-1)


def finish(global_peak, global_mass, picked):
    log_norm = global_peak + jnp.log(global_mass)
    return (log_norm - picked, log_norm * log_norm)


def body(hidden, head_weight, targets):
    vocab_index = lax.axis_index("vocab")
    vocab_share = head_weight.shape[1]
    all_tokens = lax.all_gather(hidden, "vocab", axis=1, tiled=True)
    logits = lax.psum_scatter(
        jnp.einsum("atk,kv->tav", all_tokens, head_weight, preferred_element_type=jnp.float32),
        "hid",
        scatter_dimension=0,
        tiled=True,
    )
    labels = jnp.transpose(targets)
    first_column = vocab_index * vocab_share
    local_peak, picked = peak_and_picked(logits, labels, first_column)
    global_peak = lax.pmax(local_peak, "vocab")
    local_mass = rescaled_sum(logits, global_peak)
    global_mass, picked = lax.psum((local_mass, picked), "vocab")
    entropy, squared = finish(global_peak, global_mass, picked)
    return (jnp.transpose(entropy), jnp.transpose(squared))


def solution(mesh):
    return jax.shard_map(
        body,
        mesh=mesh,
        in_specs=(P(None, "vocab", "hid"), P("hid", "vocab"), P(None, "hid")),
        out_specs=(P(None, "hid"), P(None, "hid")),
        check_vma=False,
    )
```

profile of v0, /device:TPU:0, one launch (start us, length us, event | category | flops | bytes accessed | tf_op | source)
XLA Modules:
  0.0 716.9 jit_solution(1745882738075428742)
XLA Ops:
  7.2 0.0 all-gather.2.cloned.1.call-start
  7.2 0.7 all-gather.2.cloned.1.call-update
  7.9 0.0 all-reduce.4.cloned.1.call-start
  7.9 31.4 %all-gather.2.cloned.1.call-done = bf16[2,256,1792]{2,1,0:T(8,128)(2,1)} async-done(((bf16[2,32,1792]{2,1,0:T(8,128)(2,1)}), bf16[2,256,1792]{2,1,0:T(8,128)(2,1)}) %all-gather.2.cloned.1.call-update) | async-done | bytes 1835024 | tf_op jit(solution)/shard_map/all_gather | solution.py:26
  39.3 24.7 %fusion.2 = f32[256,2,8192]{0,2,1:T(8,128)} fusion(bf16[2,256,1792]{2,1,0:T(8,128)(2,1)} %all-gather.2.cloned.1.call-done, bf16[1792,8192]{1,0:T(8,128)(2,1)} %param.4), kind=kOutput, calls=%fused_computation.2 | convolution fusion | flops 15032385536 | bytes 47972352 | tf_op jit(solution)/shard_map/atk,kv->tav/dot_general | solution.py:28
  64.0 25.4 %copy.11 = f32[256,2,8192]{2,1,0:T(2,128)} copy(f32[256,2,8192]{0,2,1:T(8,128)} %fusion.2) | data formatting | bytes 33554432 | tf_op jit(solution)/shard_map/atk,kv->tav/transpose | solution.py:28
  89.4 0.0 copy-start
  89.4 0.0 copy-start.1
  89.4 0.0 all-reduce.4.cloned.1.call-update
  89.4 0.6 copy-done
  90.1 0.1 copy.12
  90.2 0.0 copy-done.1
  90.2 0.6 dynamic-slice
  91.4 560.3 %all-reduce.4.cloned.1.call-done = f32[256,2,8192]{2,1,0:T(2,128)} async-done(((f32[256,2,8192]{2,1,0:T(2,128)}), f32[256,2,8192]{2,1,0:T(2,128)}) %all-reduce.4.cloned.1.call-update) | async-done | bytes 16777232
  651.7 3.6 dynamic-slice_reduce_fusion
  655.3 23.8 %pmax.7 = f32[64,2]{1,0:T(8,128)S(1)} all-reduce(f32[64,2]{1,0:T(8,128)S(1)} %dynamic-slice_reduce_fusion), channel_id=1, replica_groups=mesh['vocab'=8,'hid'=4] {'vocab'}, use_global_device_ids=true, to_apply=%region_2.3 | all-reduce | flops 128 | bytes 1024 | tf_op jit(solution)/shard_map/pmax | solution.py:36
  679.1 6.9 exponential_reduce_fusion
  686.0 22.7 %all-reduce.1 = (f32[64,2]{1,0:T(8,128)S(1)}, f32[64,2]{1,0:T(8,128)S(1)}) all-reduce(f32[64,2]{1,0:T(8,128)S(1)} %get-tuple-element.5, f32[64,2]{1,0:T(8,128)S(1)} %get-tuple-element.4), channel_id=1, replica_groups=mesh['vocab'=8,'hid'=4] {'vocab'}, use_global_device_ids=true, to_apply=%region_6.7 | all-reduce | flops 256 | bytes 2048 | tf_op jit(solution)/shard_map/psum | solution.py:38
  708.8 0.6 copy.13
  709.4 0.6 copy.14
  (2 shorter events, 0.0 us)
Async XLA Ops:
  7.2 32.1 %all-gather.2.cloned.1.call-start = ((), (), s32[]{:S(2)}) async-start(), calls=%async_computation | async-start | bytes 2064384 | tf_op jit(solution)/shard_map/all_gather | solution.py:26
  7.9 643.8 %all-reduce.4.cloned.1.call-start = ((), (), s32[]{:S(2)}) async-start(), calls=%async_computation.1 | async-start | bytes 33554432
  89.4 0.7 copy-start
  89.4 0.8 copy-start.1
Sparse Core Ops, SparseCore 0:
  9.9 29.3 all-gather.1
  89.5 562.1 all-reduce.3
where the time goes:
time: 718 us; the launch traced here: 717 us
  waiting for transfers between devices  592 us (82%)
  blocking collectives  46.6 us (6%)
  local copies, waits for them, and re-layouts  28 us (4%)
  matrix products  24.7 us (3%)
  between operations  14.7 us (2%)
  other arithmetic  10.5 us (1%)
    unnamed x3, waiting for transfers between devices  561 us
    all_gather x1, waiting for transfers between devices, body(): all_tokens = lax.all_gather(hidden, 'vocab', axis=1, tiled=True)  31.4 us
    transpose x1, local copies, waits for them, and re-layouts, body(): jnp.einsum('atk,kv->tav', all_tokens, head_weight, preferred_element_type...  25.4 us
    dot_general x1, matrix products, body(): jnp.einsum('atk,kv->tav', all_tokens, head_weight, preferred_element_type...  24.7 us
    pmax x1, blocking collectives, body(): global_peak = lax.pmax(local_peak, 'vocab')  23.8 us
    psum x1, blocking collectives, body(): global_mass, picked = lax.psum((local_mass, picked), 'vocab')  22.7 us
  transfers between devices with their start and end apart: 2, of which 2 were waited for; matrix products, arithmetic and copies ran while one was open for 0% of the time, Pallas kernels for 0%

commit v1 on v0

v1 whole, which is shorter than its diff:
```python
import functools

import jax
import jax.numpy as jnp
from jax import lax
from jax.experimental import pallas as pl
from jax.experimental.pallas import tpu as pltpu
from jax.sharding import PartitionSpec as P

MESH = pl.DeviceIdType.MESH
LANES = 128
SKEW = 2
LOWEST = -3.0e38
TOP = 32767.0


def kernel(
    n, nv, nj, cw,
    hidden, weight, targets,
    entropy, squared,
    rows, wbuf, came, gone, came_scale, gone_scale, part,
    labels, label_tile, peak, mass, pick, ends, mine, shared,
    w_sem, own_sem, h_send, h_recv, l_send, l_recv,
    q_send, q_recv, s_send, s_recv, e_send, e_recv, c_send, c_recv,
):
    v, me = lax.axis_index("vocab"), lax.axis_index("hid")
    groups = nv // 2
    chip, parity = v // 2, v % 2
    share = hidden.shape[1]
    block = rows.shape[1] * rows.shape[2]
    total = groups * nj
    half = nj * cw
    chains = ((me, me + 1), (n - 1 - me, me - 1))

    def w_copy(way, j):
        return pltpu.make_async_copy(
            weight.at[:, pl.ds(way * half + pl.multiple_of(j * cw, cw), cw)],
            wbuf.at[way * nj + j],
            w_sem.at[way * nj + j],
        )

    def place(b):
        return rows.at[b // 2, :, pl.ds(pl.multiple_of((b % 2) * share, share), share), :]

    own = pltpu.make_async_copy(hidden, place(v), own_sem)
    own.start()
    for j in range(2):
        for way in range(2):
            w_copy(way, j).start()

    barrier = pltpu.get_barrier_semaphore()
    for k in range(1, nv):
        pl.semaphore_signal(barrier, inc=1, device_id=((v + k) % nv, me), device_id_type=MESH)
    for k in range(1, n):
        pl.semaphore_signal(barrier, inc=1, device_id=(v, (me + k) % n), device_id_type=MESH)
    pl.semaphore_wait(barrier, nv - 1 + n - 1)

    def h_copy(slot, target):
        return pltpu.make_async_remote_copy(
            src_ref=hidden, dst_ref=place(v), send_sem=h_send.at[slot], recv_sem=h_recv.at[v],
            device_id=(target, me), device_id_type=MESH,
        )

    def h_arrival(b):
        return pltpu.make_async_remote_copy(
            src_ref=hidden, dst_ref=place(b), send_sem=h_send.at[0], recv_sem=h_recv.at[b],
            device_id=(v, me), device_id_type=MESH,
        )

    peers = [2 * chip + 1 - parity]
    for back in range(1, groups):
        other = (chip - back + groups) % groups
        peers += [2 * other + parity, 2 * other + 1 - parity]
    h_copies = [h_copy(slot, target) for slot, target in enumerate(peers)]
    for copy in h_copies:
        copy.start()

    finals = (n - 1, 0)

    def l_copy(e):
        return pltpu.make_async_remote_copy(
            src_ref=targets, dst_ref=labels.at[me], send_sem=l_send.at[e], recv_sem=l_recv.at[me],
            device_id=(v, finals[e]), device_id_type=MESH,
        )

    for e in range(2):
        @pl.when(me != finals[e])
        def _():
            l_copy(e).start()

        @pl.when(me == finals[e])
        def _():
            labels[me] = targets[...]

    is_end = jnp.logical_or(me == 0, me == n - 1)

    def message(way, k, target):
        data = pltpu.make_async_remote_copy(
            src_ref=gone.at[way, k], dst_ref=came.at[way, k],
            send_sem=q_send.at[way, k], recv_sem=q_recv.at[way, k],
            device_id=(v, target), device_id_type=MESH,
        )
        scale = pltpu.make_async_remote_copy(
            src_ref=gone_scale.at[way, k], dst_ref=came_scale.at[way, k],
            send_sem=s_send.at[way, k], recv_sem=s_recv.at[way, k],
            device_id=(v, target), device_id_type=MESH,
        )
        return data, scale

    def send_end(e, g):
        return pltpu.make_async_remote_copy(
            src_ref=ends.at[g], dst_ref=mine.at[e], send_sem=e_send.at[g], recv_sem=e_recv.at[e],
            device_id=(v, g), device_id_type=MESH,
        )

    def statistics(way, g, j):
        @pl.when(j == 0)
        def _():
            line = labels[g]
            line = jnp.concatenate([line[0:1, :], line[1:2, :]], axis=1)
            label_tile[...] = jnp.transpose(jnp.broadcast_to(line, (block, block)))
            peak[...] = jnp.full_like(peak, LOWEST)
            mass[...] = jnp.zeros_like(mass)
            pick[...] = jnp.zeros_like(pick)

        x = part[way]
        pieces = [x[:, c * LANES : (c + 1) * LANES] for c in range(cw // LANES)]
        old = peak[...]
        new = functools.reduce(jnp.maximum, pieces, old)
        peak[...] = new
        mass[...] = mass[...] * jnp.exp(old - new) + sum(jnp.exp(piece - new) for piece in pieces)
        first = v * (2 * half) + way * half + j * cw
        offset = label_tile[...] - first
        lane = lax.broadcasted_iota(jnp.int32, (block, LANES), 1)
        found = pick[...]
        for c, piece in enumerate(pieces):
            found = found + jnp.where(offset == lane + c * LANES, piece, 0.0)
        pick[...] = found

        @pl.when(j == nj - 1)
        def _():
            tall = jnp.transpose(peak[...])
            top = jnp.max(tall, axis=0, keepdims=True)
            weight_sum = jnp.sum(jnp.transpose(mass[...]) * jnp.exp(tall - top), axis=0, keepdims=True)
            chosen = jnp.sum(jnp.transpose(pick[...]), axis=0, keepdims=True)
            ends[g] = jnp.concatenate([top, weight_sum, chosen, jnp.zeros((5, block), jnp.float32)], axis=0)

            @pl.when(g != me)
            def _():
                send_end(way, g).start()

            @pl.when(g == me)
            def _():
                mine[way] = ends[g]

    def process(way, k):
        pos, target = chains[way]
        rb, j = k // nj, k % nj
        g = (chip + rb) % groups

        @pl.when(rb == 0)
        def _():
            @pl.when(j + 2 < nj)
            def _():
                w_copy(way, j + 2).start()

            w_copy(way, j).wait()

        a = rows[g].reshape(block, rows.shape[3])
        part[way] = jnp.dot(a, wbuf[way * nj + j], preferred_element_type=jnp.float32)

        @pl.when(pos > 0)
        def _():
            for copy in message(way, k, me):
                copy.wait_recv()
            part[way] += came[way, k].astype(jnp.int32).astype(jnp.float32) * came_scale[way, k]

        @pl.when(pos < n - 1)
        def _():
            x = part[way]
            largest = jnp.maximum(jnp.max(jnp.abs(x), axis=0, keepdims=True), 1e-30)
            gone_scale[way, k] = largest * (1.0 / TOP)
            gone[way, k] = jnp.round(x * (TOP / largest)).astype(jnp.int32).astype(jnp.int16)
            for copy in message(way, k, target):
                copy.start()

        @pl.when(pos == n - 1)
        def _():
            statistics(way, g, j)

    nearest = jnp.minimum(me, n - 1 - me)
    own.wait()

    @pl.when(is_end)
    def _():
        for z in range(n):
            @pl.when(me != z)
            def _():
                pltpu.make_async_remote_copy(
                    src_ref=targets, dst_ref=labels.at[z], send_sem=l_send.at[0], recv_sem=l_recv.at[z],
                    device_id=(v, me), device_id_type=MESH,
                ).wait_recv()

    def step(i, carry):
        lead = i - nearest * SKEW

        @pl.when(jnp.logical_and(lead >= 0, jnp.logical_and(lead < total, lead % nj == 0)))
        def _():
            rb = lead // nj
            g = (chip + rb) % groups
            for side in range(2):
                @pl.when(2 * g + side != v)
                def _():
                    h_arrival(2 * g + side).wait_recv()

        for way in range(2):
            k = i - chains[way][0] * SKEW

            @pl.when(jnp.logical_and(k >= 0, k < total))
            def _():
                process(way, k)

        return carry

    lax.fori_loop(0, total + (n - 1) * SKEW, step, 0)

    for e in range(2):
        @pl.when(me != finals[e])
        def _():
            send_end(e, me).wait_recv()

    def merge(tiles):
        top = functools.reduce(jnp.maximum, [t[0:1] for t in tiles])
        weight_sum = sum(t[1:2] * jnp.exp(t[0:1] - top) for t in tiles)
        chosen = sum(t[2:3] for t in tiles)
        return top, weight_sum, chosen

    top, weight_sum, chosen = merge([mine[0], mine[1]])
    shared[v] = jnp.concatenate([top, weight_sum, chosen, jnp.zeros((5, block), jnp.float32)], axis=0)

    def c_copy(slot, source, target):
        return pltpu.make_async_remote_copy(
            src_ref=shared.at[source], dst_ref=shared.at[source], send_sem=c_send.at[slot], recv_sem=c_recv.at[source],
            device_id=(target, me), device_id_type=MESH,
        )

    for k in range(1, nv):
        c_copy(k - 1, v, (v + k) % nv).start()
    for k in range(1, nv):
        c_copy(0, (v + k) % nv, v).wait_recv()
    top, weight_sum, chosen = merge([shared[k] for k in range(nv)])
    norm = top + jnp.log(weight_sum)
    loss, square = norm - chosen, norm * norm
    width = block // 2
    for a in range(2):
        entropy[a : a + 1, :] = loss[:, a * width : (a + 1) * width]
        squared[a : a + 1, :] = square[:, a * width : (a + 1) * width]

    for copy in h_copies:
        copy.wait_send()
    for e in range(2):
        @pl.when(me != finals[e])
        def _():
            l_copy(e).wait_send()
    for way in range(2):
        pos, target = chains[way]

        @pl.when(pos < n - 1)
        def _():
            def drain(k, carry):
                for copy in message(way, k, target):
                    copy.wait_send()
                return carry

            lax.fori_loop(0, total, drain, 0)

        @pl.when(pos == n - 1)
        def _():
            for g in range(groups):
                @pl.when(me != g)
                def _():
                    send_end(way, g).wait_send()
    for k in range(1, nv):
        c_copy(k - 1, v, (v + k) % nv).wait_send()


def body(n, nv, hidden, head_weight, targets):
    depths, share, width = hidden.shape
    columns = head_weight.shape[1]
    groups = nv // 2
    assert groups == n and depths == 2 and depths * 2 * share == LANES
    cw = min(512, columns // 2)
    nj = columns // 2 // cw
    total = groups * nj
    block = depths * 2 * share
    vmem, anywhere = pl.BlockSpec(memory_space=pltpu.VMEM), pl.BlockSpec(memory_space=pl.ANY)
    dma = pltpu.SemaphoreType.DMA
    return pl.pallas_call(
        functools.partial(kernel, n, nv, nj, cw),
        out_shape=[jax.ShapeDtypeStruct(targets.shape, jnp.float32)] * 2,
        in_specs=[anywhere, anywhere, vmem],
        out_specs=[vmem, vmem],
        scratch_shapes=[
            pltpu.VMEM((groups, depths, 2 * share, width), hidden.dtype),
            pltpu.VMEM((2 * nj, width, cw), head_weight.dtype),
            pltpu.VMEM((2, total, block, cw), jnp.int16),
            pltpu.VMEM((2, total, block, cw), jnp.int16),
            pltpu.VMEM((2, total, 1, cw), jnp.float32),
            pltpu.VMEM((2, total, 1, cw), jnp.float32),
            pltpu.VMEM((2, block, cw), jnp.float32),
            pltpu.VMEM((n,) + targets.shape, jnp.int32),
            pltpu.VMEM((block, LANES), jnp.int32),
            pltpu.VMEM((block, LANES), jnp.float32),
            pltpu.VMEM((block, LANES), jnp.float32),
            pltpu.VMEM((block, LANES), jnp.float32),
            pltpu.VMEM((groups, 8, block), jnp.float32),
            pltpu.VMEM((2, 8, block), jnp.float32),
            pltpu.VMEM((nv, 8, block), jnp.float32),
            dma((2 * nj,)), dma, dma((nv - 1,)), dma((nv,)), dma((2,)), dma((n,)),
            dma((2, total)), dma((2, total)), dma((2, total)), dma((2, total)),
            dma((groups,)), dma((2,)), dma((nv - 1,)), dma((nv,)),
        ],
        compiler_params=pltpu.CompilerParams(
            collective_id=0, has_side_effects=True, vmem_limit_bytes=60 * 1024 * 1024
        ),
    )(hidden, head_weight, targets)


def solution(mesh):
    return jax.shard_map(
        functools.partial(body, mesh.shape["hid"], mesh.shape["vocab"]),
        mesh=mesh,
        in_specs=(P(None, "vocab", "hid"), P("hid", "vocab"), P(None, "hid")),
        out_specs=(P(None, "hid"), P(None, "hid")),
        check_vma=False,
    )
```

time: 718 us -> 125 us (0.17)
  waiting for transfers between devices: 592 us -> 0 us
  Pallas kernels: 0 us -> 122 us
  blocking collectives: 46.6 us -> 0 us
  local copies, waits for them, and re-layouts: 28 us -> 2.44 us
  matrix products: 24.7 us -> 0 us
  between operations: 14.7 us -> 0.64 us
  other arithmetic: 10.5 us -> 0 us
    unnamed x3 -> x0, waiting for transfers between devices: 561 us -> none
    pallas_call x0 -> x1, Pallas kernels: none -> 122 us  [body(): pl.pallas_call(functools.partial(kernel, n, nv, nj, cw), out_shape=[jax.S...]
    all_gather x1 -> x0, waiting for transfers between devices: 31.4 us -> none  [body(): all_tokens = lax.all_gather(hidden, 'vocab', axis=1, tiled=True)]
    transpose x2 -> x0, local copies, waits for them, and re-layouts: 25.5 us -> none  [the longest x1 25.4 us: body(): jnp.einsum('atk,kv->tav', all_tokens, head_weight, preferred_element_type...]
    dot_general x1 -> x0, matrix products: 24.7 us -> none  [body(): jnp.einsum('atk,kv->tav', all_tokens, head_weight, preferred_element_type...]
    pmax x1 -> x0, blocking collectives: 23.8 us -> none  [body(): global_peak = lax.pmax(local_peak, 'vocab')]
    psum x1 -> x0, blocking collectives: 22.7 us -> none  [body(): global_mass, picked = lax.psum((local_mass, picked), 'vocab')]
  transfers between devices with their start and end apart: 2 -> 0, of which waited for: 2 -> 0; matrix products, arithmetic and copies ran while one was open for 0% -> 0% of each run, Pallas kernels for 0% -> 0%
where the time goes in v1:
time: 125 us
  Pallas kernels  122 us (98%)
  local copies, waits for them, and re-layouts  2.44 us (2%)
    pallas_call x1, Pallas kernels, body(): pl.pallas_call(functools.partial(kernel, n, nv, nj, cw), out_shape=[jax.S...  122 us

profile of v1, /device:TPU:0, one launch (start us, length us, event | category | flops | bytes accessed | tf_op | source)
XLA Modules:
  0.0 125.1 jit_solution(2548655534379009224)
XLA Ops:
  0.6 122.0 %shard_map.50 = (f32[2,64]{1,0:T(2,128)}, f32[2,64]{1,0:T(2,128)}) custom-call(bf16[2,32,1792]{2,1,0:T(8,128)(2,1)} %hidden.1, bf16[1792,8192]{1,0:T(8,128)(2,1)} %weight.1, s32[2,64]{1,0:T(2,128)} %targets.1), custom_call_target="tpu_custom_call" | custom-call | tf_op jit(solution)/shard_map/pallas_call | solution.py:298
  122.6 1.2 copy.7
  123.8 1.2 copy.8

commit v2 on v1

--- a/solution.py
+++ b/solution.py
@@ -9,7 +9,7 @@
 
 MESH = pl.DeviceIdType.MESH
 LANES = 128
-SKEW = 2
+SKEW = 4
 LOWEST = -3.0e38
 TOP = 32767.0
 
@@ -289,7 +289,7 @@
     columns = head_weight.shape[1]
     groups = nv // 2
     assert groups == n and depths == 2 and depths * 2 * share == LANES
-    cw = min(512, columns // 2)
+    cw = min(256, columns // 2)
     nj = columns // 2 // cw
     total = groups * nj
     block = depths * 2 * share

time: 125 us -> 127 us (1.016)
    pallas_call x1, Pallas kernels: 122 us -> 123 us  [body(): pl.pallas_call(functools.partial(kernel, n, nv, nj, cw), out_shape=[jax.S...]
where the time goes in v2:
time: 127 us; the launch traced here: 126 us
  Pallas kernels  123 us (97%)
  local copies, waits for them, and re-layouts  2.44 us (2%)
    pallas_call x1, Pallas kernels, body(): pl.pallas_call(functools.partial(kernel, n, nv, nj, cw), out_shape=[jax.S...  123 us

profile of v2, /device:TPU:0, one launch (start us, length us, event | category | flops | bytes accessed | tf_op | source)
XLA Modules:
  0.0 126.4 jit_solution(317268546816947442)
XLA Ops:
  0.6 123.3 %shard_map.50 = (f32[2,64]{1,0:T(2,128)}, f32[2,64]{1,0:T(2,128)}) custom-call(bf16[2,32,1792]{2,1,0:T(8,128)(2,1)} %hidden.1, bf16[1792,8192]{1,0:T(8,128)(2,1)} %weight.1, s32[2,64]{1,0:T(2,128)} %targets.1), custom_call_target="tpu_custom_call" | custom-call | tf_op jit(solution)/shard_map/pallas_call | solution.py:298
  124.0 1.2 copy.7
  125.2 1.2 copy.8
